TPU v7x, 256 devices: a whole 4x4x8 slice. The times are simulated.
256 devices in a mesh: rep: 4 (over z_hi), tok: 4 (over z_lo, core), voc: 16 (over x, y).
Axes of the slice: x: 4, y: 4, z: 8 (z_hi: 4, z_lo: 2; z = z_hi * 2 + z_lo), core: 2. Of those that a mesh axis runs over, the one named last changes fastest.
Arguments:
- hidden: bfloat16 [4, 512, 4096], P('rep', ('tok', 'voc')), may hold values from -500 to 500
- targets: int32 [4, 512], P('rep', ('tok', 'voc')), may hold values from 0 to 65535
- unembed: bfloat16 [4, 65536, 4096], P('rep', ('tok', 'voc')), may hold values from -1 to 1
- outer_weight: float32 [8192, 4096], P(('tok', 'voc'), 'rep'), may hold values from -0.9 to 0.9
- momentum: float32 [8192, 4096], P(('tok', 'voc'), 'rep'), may hold values from -0.18 to 0.18
Outputs:
- token_loss: float32 [4, 512], P('rep', ('tok', 'voc'))
- hidden_grad: float32 [4, 512, 4096], P('rep', ('tok', 'voc'))
- new_outer: float32 [8192, 4096], P(('tok', 'voc'), 'rep')
- new_momentum: float32 [8192, 4096], P(('tok', 'voc'), 'rep')
- next_inner: bfloat16 [8192, 4096], P(('tok', 'voc'))
All inputs are finite; a program needn't handle non-finite values.
Results may differ from a plain program's by a relative error of at most 0.0085.
Values may be sent and summed in bfloat16 or wider, within the bound.
No kernel may reach another device: no remote copies, remote signals or barrier semaphores. Data moves between devices by JAX's collectives and lax.ppermute only.
A program may use at most 64 MiB of HBM per device.

v0:
```python
import jax
import jax.numpy as jnp
from jax import lax
from jax.sharding import Mesh
from jax.sharding import PartitionSpec as P

TOK = ("tok_0", "tok_1")
VOC = ("voc_0", "voc_1")
TOK_VOC = ("tok_0", "tok_1", "voc_0", "voc_1")
inner_rate = 0.5
outer_rate = 0.7
momentum_coef = 0.9


def laid_out(pieces, dim):
    dims = list(pieces.shape[1:])
    dims[dim] *= pieces.shape[0]
    return jnp.moveaxis(pieces, 0, dim).reshape(dims)


def stacked_from(value, axes, turns):
    pieces = value[None]
    for k in turns:
        pieces = lax.all_gather(pieces, axes[k], axis=0, tiled=True)
    carried = [lax.axis_size(axes[k]) for k in reversed(turns)]
    pieces = pieces.reshape(*carried, *value.shape)
    turned = sorted(range(len(turns)), key=lambda place: turns[len(turns) - 1 - place])
    return pieces.transpose(*turned, *range(len(turns), pieces.ndim)).reshape(-1, *value.shape)


def gathered_by_axis(value, axes, turns, dim):
    return laid_out(stacked_from(value, axes, turns), dim)


def sent_to_all(value, axis):
    devices = lax.axis_size(axis)
    return lax.all_to_all(
        jnp.broadcast_to(value[None], (devices, *value.shape)), axis, 0, 0, tiled=True
    )


def collected_together(value, axis):
    leaves = jax.tree.leaves(value)
    turns = sorted(range(len(leaves)), key=lambda k: -leaves[k].size)
    width = (1, *leaves[turns[0]].shape)[-1]
    lines = [
        jnp.pad(leaves[k].reshape(-1), (0, -leaves[k].size % width)).reshape(-1, width)
        for k in turns
    ]
    both, at, found = (sent_to_all(jnp.concatenate(lines), axis), 0, {})
    for k, line in zip(turns, lines):
        piece = both[:, at : at + len(line)].reshape(len(both), -1)
        found[k] = piece[:, : leaves[k].size].reshape(-1, *leaves[k].shape)
        at += len(line)
    numbers = iter(range(len(leaves)))
    return jax.tree.map(lambda _: found[next(numbers)], value)


def combined_pairwise(pieces, combine):
    while len(jax.tree.leaves(pieces)[0]) > 1:
        pieces = jax.vmap(combine)(
            *(jax.tree.map(lambda part: part[side::2], pieces) for side in (0, 1))
        )
    return jax.tree.map(lambda part: part[0], pieces)


def combined_all(value, axis, combine):
    pieces = collected_together(value, axis)
    return combined_pairwise(pieces, combine)


def split_up(value, dim, devices):
    dims = value.shape
    pieces = value.reshape(*dims[:dim], devices, dims[dim] // devices, *dims[dim + 1 :])
    return jnp.moveaxis(pieces, dim, 0)


def sum_at_owner(value, axis, dim):
    devices = lax.axis_size(axis)
    pieces = lax.all_to_all(split_up(value, dim, devices), axis, 0, 0, tiled=True)
    return jnp.sum(pieces.astype(jnp.float32), axis=0)


def sent_and_summed(value, axis, dim):
    pieces = split_up(value, dim, lax.axis_size(axis))
    arrived = lax.all_to_all(pieces, axis, split_axis=0, concat_axis=0, tiled=True)
    return arrived.sum(axis=0)


def gather_directly(value, axis, dim):
    pieces = sent_to_all(value, axis)
    return laid_out(pieces, dim)


def combine_stats(earlier, latter):
    row_top = jnp.maximum(earlier[0], latter[0])
    row_total = earlier[1] * jnp.exp(earlier[0] - row_top) + latter[1] * jnp.exp(
        latter[0] - row_top
    )
    return (row_top, row_total, earlier[2] + latter[2])


def nesterov(outer_part, momentum_part, mean_final):
    pseudo_grad = outer_part - mean_final
    moved_momentum = momentum_coef * momentum_part + pseudo_grad
    moved_outer = outer_part - outer_rate * (pseudo_grad + momentum_coef * moved_momentum)
    return (moved_outer, moved_momentum)


def per_device(hidden, targets, unembed, outer_weight, momentum):
    weights = unembed[0]
    vocab_rows, model_width = weights.shape
    tok_rows = hidden.shape[1]
    slab_rows = outer_weight.shape[0]
    logit_scale = model_width ** (-0.5)
    group_index = lax.axis_index(TOK) * lax.axis_size(VOC) + lax.axis_index(VOC)
    every_hidden, every_target = (
        gathered_by_axis(hidden[0], TOK_VOC, (0, 2, 3, 1), 0),
        gathered_by_axis(targets[0], TOK_VOC, (0, 2, 3, 1), 0),
    )
    logits = (
        jnp.einsum("td,vd->tv", every_hidden, weights, preferred_element_type=jnp.float32)
        * logit_scale
    )
    columns = group_index * vocab_rows + lax.broadcasted_iota(jnp.int32, (1, vocab_rows), 1)
    onehot = every_target[:, None] == columns
    target_part = jnp.sum(jnp.where(onehot, logits, 0.0), axis=1)
    local_top = jnp.max(logits, axis=1)
    local_total = jnp.sum(jnp.exp(logits - local_top[:, None]), axis=1)
    row_top, row_total, target_logit = combined_all(
        (local_top, local_total, target_part), TOK_VOC, combine_stats
    )
    log_total = row_top + jnp.log(row_total)
    every_loss = log_total - target_logit
    token_loss = lax.dynamic_slice_in_dim(every_loss, group_index * tok_rows, tok_rows)[None]
    errors = (jnp.exp(logits - log_total[:, None]) - onehot.astype(jnp.float32)).astype(
        jnp.bfloat16
    )
    partial_grad = jnp.dot(errors, weights, preferred_element_type=jnp.float32) * logit_scale
    tok_count = lax.axis_size(TOK)
    split_partial = partial_grad.reshape(tok_count, partial_grad.shape[0] // tok_count, model_width)
    first_section = lax.psum_scatter(
        split_partial.astype(jnp.bfloat16), TOK, scatter_dimension=0, tiled=True
    ).astype(jnp.float32)
    token_grad = sum_at_owner(first_section[0].astype(jnp.bfloat16), VOC, 0)
    slab_errors = errors[:, :slab_rows]
    slab_grad = (
        jnp.einsum("tv,td->vd", slab_errors, every_hidden, preferred_element_type=jnp.float32)
        * logit_scale
    )
    final_slab = weights[:slab_rows].astype(jnp.float32) - inner_rate * slab_grad
    replicas = lax.axis_size("rep")
    mean_final = sent_and_summed(final_slab, "rep", 1) / replicas
    new_outer, new_momentum = nesterov(outer_weight, momentum, mean_final)
    next_inner = gather_directly(new_outer.astype(jnp.bfloat16), "rep", 1)
    return (token_loss, token_grad[None], new_outer, new_momentum, next_inner)


def solution(mesh):
    finer = Mesh(
        mesh.devices.reshape(mesh.shape["rep"], 2, 2, 4, 4),
        ("rep", "tok_0", "tok_1", "voc_0", "voc_1"),
    )
    in_specs = (
        P("rep", TOK_VOC, None),
        P("rep", TOK_VOC),
        P("rep", TOK_VOC, None),
        P(TOK_VOC, "rep"),
        P(TOK_VOC, "rep"),
    )
    out_specs = (
        P("rep", TOK_VOC),
        P("rep", TOK_VOC, None),
        P(TOK_VOC, "rep"),
        P(TOK_VOC, "rep"),
        P(TOK_VOC, None),
    )
    return jax.shard_map(
        per_device, mesh=finer, in_specs=in_specs, out_specs=out_specs, check_vma=False
    )
```

profile of v0, /device:TPU:32, one launch (start us, length us, event | category | flops | bytes accessed | tf_op | source)
XLA Modules:
  0.0 273.8 jit_solution(8645749955817782330)
XLA Ops:
  7.2 5.1 %all_gather.24 = bf16[2,8,4096]{2,1,0:T(8,128)(2,1)S(1)} all-gather(bf16[1,8,4096]{2,1,0:T(8,128)(2,1)} %param.5), channel_id=1, replica_groups=mesh['rep'=4,'tok_0'=2,'tok_1'=2,'voc_0'=4,'voc_1'=4] {'tok_0'}, dimensions={0}, use_global_device_ids=true | all-gather | bytes 196608 | tf_op jit(solution)/shard_map/all_gather | solution.py:24
  12.4 14.2 %all_gather.25 = bf16[8,8,4096]{2,1,0:T(8,128)(2,1)} all-gather(bf16[2,8,4096]{2,1,0:T(8,128)(2,1)S(1)} %all_gather.24), channel_id=1, replica_groups=mesh['rep'=4,'tok_0'=2,'tok_1'=2,'voc_0'=4,'voc_1'=4] {'voc_0'}, dimensions={0}, use_global_device_ids=true | all-gather | bytes 655360 | tf_op jit(solution)/shard_map/all_gather | solution.py:24
  26.6 35.6 %all-gather.6.cloned.1.call-done = bf16[32,8,4096]{2,1,0:T(8,128)(2,1)} async-done(((bf16[8,8,4096]{2,1,0:T(8,128)(2,1)}), bf16[32,8,4096]{2,1,0:T(8,128)(2,1)}) %all-gather.6.cloned.1.call-update) | async-done | bytes 2097168 | tf_op jit(solution)/shard_map/all_gather | solution.py:24
  62.2 4.2 %all-gather = s32[2,1,8]{2,1,0:T(1,128)S(1)} all-gather(s32[1,1,8]{2,1,0:T(1,128)S(1)} %bitcast.74), channel_id=1, replica_groups=mesh['rep'=4,'tok_0'=2,'tok_1'=2,'voc_0'=4,'voc_1'=4] {'tok_0'}, dimensions={0}, use_global_device_ids=true | all-gather | bytes 96 | tf_op jit(solution)/shard_map/all_gather | solution.py:24
  66.5 9.7 %all-gather.1 = s32[4,2,8]{2,1,0:T(2,128)S(1)} all-gather(s32[1,2,8]{2,1,0:T(2,128)S(1)} %bitcast.73), channel_id=1, replica_groups=mesh['rep'=4,'tok_0'=2,'tok_1'=2,'voc_0'=4,'voc_1'=4] {'voc_0'}, dimensions={0}, use_global_device_ids=true | all-gather | bytes 320 | tf_op jit(solution)/shard_map/all_gather | solution.py:24
  76.1 12.0 %all_gather.30 = s32[32,8]{1,0:T(8,128)S(1)} all-gather(s32[8,8]{1,0:T(8,128)S(1)} %bitcast.68), channel_id=1, replica_groups=mesh['rep'=4,'tok_0'=2,'tok_1'=2,'voc_0'=4,'voc_1'=4] {'voc_1'}, dimensions={0}, use_global_device_ids=true | all-gather | bytes 1280 | tf_op jit(solution)/shard_map/all_gather | solution.py:24
  88.2 1.8 all-gather.2
  90.0 0.1 copy.23
  90.1 0.1 eq.15
  90.3 2.8 %copy.21 = bf16[2,2,4,4,8,4096]{5,4,3,2,1,0:T(8,128)(2,1)S(1)} copy(bf16[2,2,4,4,8,4096]{5,4,0,2,3,1:T(8,128)(2,1)} %bitcast.57) | data formatting | bytes 8388608 | tf_op jit(solution)/shard_map/transpose | solution.py:28
  93.1 3.3 %copy-done.2 = bf16[1,1024,4096]{2,1,0:T(8,128)(2,1)S(1)} copy-done((bf16[1,1024,4096]{2,1,0:T(8,128)(2,1)S(1)}, bf16[1,1024,4096]{2,1,0:T(8,128)(2,1)}, u32[]{:S(2)}) %copy-start.2) | copy-done | bytes 8388632
  96.4 4.6 %multiply_reduce_fusion = (f32[512]{0:T(512)S(1)}, f32[512,1024]{1,0:T(8,128)S(1)}) fusion(bf16[512,4096]{1,0:T(8,128)(2,1)S(1)} %bitcast.53, bf16[1,1024,4096]{2,1,0:T(8,128)(2,1)S(1)} %copy-done.2), kind=kOutput, calls=%fused_computation.15 | convolution fusion | flops 4296015360 | bytes 14682112 | tf_op jit(solution)/shard_map/td,vd->tv/dot_general | solution.py:122
  101.1 0.9 exponential_reduce_fusion
  102.0 0.1 broadcast_in_dim.13
  102.1 16.1 %all_to_all.20 = f32[64,3,512]{2,1,0:T(4,128)S(1)} all-to-all(f32[64,3,512]{2,1,0:T(4,128)S(1)} %broadcast_in_dim.13), channel_id=1, replica_groups=mesh['rep'=4,'tok_0'=2,'tok_1'=2,'voc_0'=4,'voc_1'=4] {'tok_0','tok_1','..., dimensions={0} | all-to-all | bytes 786432 | tf_op jit(solution)/shard_map/all_to_all | solution.py:37
  118.2 0.3 fusion.14
  119.1 0.6 fusion.9
  119.7 9.4 %multiply_convert_fusion = bf16[512,4096]{1,0:T(8,128)(2,1)} fusion(bf16[512,1024]{1,0:T(8,128)(2,1)S(1)} %fusion.9, bf16[1,1024,4096]{2,1,0:T(8,128)(2,1)} %param.7), kind=kOutput, calls=%fused_computation.4 | convolution fusion | flops 4299161600 | bytes 13631488 | tf_op jit(solution)/shard_map/dot_general | solution.py:139
  129.2 3.3 %fusion.6 = f32[128,4096]{1,0:T(8,128)S(1)} fusion(bf16[512,4096]{1,0:T(8,128)(2,1)} %bitcast.54, bf16[1,1024,4096]{2,1,0:T(8,128)(2,1)} %param.7, bf16[512,1024]{1,0:T(8,128)(2,1)S(1)} %fusion.9), kind=kOutput, calls=%fused_computation.6 | convolution fusion | flops 538443776 | bytes 7471104 | tf_op jit(solution)/shard_map/tv,td->vd/dot_general | solution.py:148
  132.4 0.2 copy.37
  132.7 79.2 %all_to_all.21 = f32[4,128,1024]{2,1,0:T(8,128)S(1)} all-to-all(f32[4,128,1024]{2,1,0:T(8,128)S(1)} %bitcast.55), channel_id=1, replica_groups=mesh['rep'=4,'tok_0'=2,'tok_1'=2,'voc_0'=4,'voc_1'=4] {'rep'}, dimensions={0} | all-to-all | bytes 4194304 | tf_op jit(solution)/shard_map/all_to_all | solution.py:86
  211.9 0.2 reduce_sum.39
  212.1 0.8 copy-done.1
  212.9 2.2 fusion.13
  215.1 0.1 broadcast_in_dim.28
  215.3 30.5 %all_to_all.22 = bf16[4,128,1024]{2,1,0:T(8,128)(2,1)S(1)} all-to-all(bf16[4,128,1024]{2,1,0:T(8,128)(2,1)S(1)} %broadcast_in_dim.28), channel_id=1, replica_groups=mesh['rep'=4,'tok_0'=2,'tok_1'=2,'voc_0'=4,'voc_1'=4] {'rep'}, dimensions={0} | all-to-all | bytes 2097152 | tf_op jit(solution)/shard_map/all_to_all | solution.py:37
  245.7 3.7 %all-to-all-start.1 = ((bf16[16,8,4096]{2,1,0:T(8,128)(2,1)}), bf16[16,8,4096]{2,1,0:T(8,128)(2,1)S(1)}, u32[]{:S(2)}, u32[]{:S(2)}) async-start(bf16[16,8,4096]{2,1,0:T(8,128)(2,1)} %bitcast.60), calls=%async_computation.2 | async-start | bytes 2097152 | tf_op jit(solution)/shard_map/all_to_all | solution.py:80
  249.7 0.6 dynamic-slice_bitcast_fusion
  250.3 0.7 copy.27
  251.0 1.3 copy.28
  252.3 14.2 %all-to-all-done.1 = bf16[16,8,4096]{2,1,0:T(8,128)(2,1)S(1)} async-done(((bf16[16,8,4096]{2,1,0:T(8,128)(2,1)}), bf16[16,8,4096]{2,1,0:T(8,128)(2,1)S(1)}, u32[]{:S(2)}, u32[]{:S(2)}) %all-to-all-start.1) | async-done | bytes 1048608 | tf_op jit(solution)/shard_map/all_to_all | solution.py:80
  266.5 0.8 convert_reduce_fusion
  (63 shorter events, 1.2 us)
Async XLA Ops:
  7.2 55.1 %copy-start.3 = (s32[1,8]{1,0:T(1,128)S(1)}, s32[1,8]{1,0:T(1,128)}, u32[]{:S(2)}) copy-start(s32[1,8]{1,0:T(1,128)} %param.6) | copy-start | bytes 100
  7.2 55.0 %all-gather.6.cloned.1.call-start = ((), (), s32[]{:S(2)}) async-start(), calls=%async_computation.5 | async-start | bytes 2621440 | tf_op jit(solution)/shard_map/all_gather | solution.py:24
  26.5 63.7 %all-gather.8.cloned.1.call-start = ((), (), s32[]{:S(2)}) async-start(), calls=%async_computation.6 | async-start | bytes 6291456 | tf_op jit(solution)/shard_map/all_gather | solution.py:24
  62.2 183.6 %reduce-scatter.2.cloned.1.call-start = ((), (), s32[]{:S(2)}) async-start(), calls=%async_computation.7 | async-start | bytes 5242880 | tf_op jit(solution)/shard_map/reduce_scatter | solution.py:142
  90.3 6.2 %copy-start.2 = (bf16[1,1024,4096]{2,1,0:T(8,128)(2,1)S(1)}, bf16[1,1024,4096]{2,1,0:T(8,128)(2,1)}, u32[]{:S(2)}) copy-start(bf16[1,1024,4096]{2,1,0:T(8,128)(2,1)} %param.7) | copy-start | bytes 25165828
  93.1 8.0 %copy-start = (bf16[2,2,4,4,8,4096]{5,4,3,2,1,0:T(8,128)(2,1)}, bf16[2,2,4,4,8,4096]{5,4,3,2,1,0:T(8,128)(2,1)S(1)}, u32[]{:S(2)}) copy-start(bf16[2,2,4,4,8,4096]{5,4,3,2,1,0:T(8,128)(2,1)S(1)} %copy.21) | copy-start | bytes 12582916
  211.9 1.0 copy-start.1
  245.7 20.8 %all-to-all-start.1 = ((bf16[16,8,4096]{2,1,0:T(8,128)(2,1)}), bf16[16,8,4096]{2,1,0:T(8,128)(2,1)S(1)}, u32[]{:S(2)}, u32[]{:S(2)}) async-start(bf16[16,8,4096]{2,1,0:T(8,128)(2,1)} %bitcast.60), calls=%async_computation.2 | async-start | bytes 2097152 | tf_op jit(solution)/shard_map/all_to_all | solution.py:80
Sparse Core Ops, SparseCore 0:
  26.7 35.4 all-gather.5
  63.9 19.0 all-gather.7
  129.3 89.2 reduce-scatter.1
where the time goes:
time: 274 us
  blocking collectives  173 us (63%)
  waiting for transfers between devices  49.9 us (18%)
  matrix products  17.3 us (6%)
  between operations  14 us (5%)
  local copies, waits for them, and re-layouts  11.2 us (4%)
  other arithmetic  4.85 us (2%)
  starting transfers between devices  3.77 us (1%)
    all_to_all x1, blocking collectives, sent_and_summed(): lax.all_to_all(pieces, axis, split_axis=0, concat_axis=0, tiled=True)  79.2 us
    all_gather x6, blocking collectives, stacked_from(): pieces = lax.all_gather(pieces, axes[k], axis=0, tiled=True)  47 us
    all_to_all x2, blocking collectives, sent_to_all(): lax.all_to_all(jnp.broadcast_to(value[None], (devices, *value.shape)), ax...  46.6 us
    all_gather x2, waiting for transfers between devices, stacked_from(): pieces = lax.all_gather(pieces, axes[k], axis=0, tiled=True)  35.6 us
    all_to_all x1, waiting for transfers between devices, sum_at_owner(): lax.all_to_all(split_up(value, dim, devices), axis, 0, 0, tiled=True)  14.2 us
    dot_general x1, matrix products, per_device(): jnp.dot(errors, weights, preferred_element_type=jnp.float32) * logit_scale  9.42 us
    unnamed x11, local copies, waits for them, and re-layouts  5.56 us
  transfers between devices with their start and end apart: 4, of which 2 were waited for; matrix products, arithmetic and copies ran while one was open for 3% of the time, Pallas kernels for 0%

commit v1 on v0

--- a/solution.py
+++ b/solution.py
@@ -21,7 +21,10 @@
 def stacked_from(value, axes, turns):
     pieces = value[None]
     for k in turns:
-        pieces = lax.all_gather(pieces, axes[k], axis=0, tiled=True)
+        size = lax.axis_size(axes[k])
+        blocks = jnp.stack([pieces for _ in range(size)])
+        blocks = lax.all_to_all(blocks, axes[k], split_axis=0, concat_axis=0)
+        pieces = jnp.concatenate(blocks, axis=0)
     carried = [lax.axis_size(axes[k]) for k in reversed(turns)]
     pieces = pieces.reshape(*carried, *value.shape)
     turned = sorted(range(len(turns)), key=lambda place: turns[len(turns) - 1 - place])

time: 274 us -> 278 us (1.015)
  starting transfers between devices: 3.77 us -> 11.8 us
  waiting for transfers between devices: 49.9 us -> 42.6 us
    all_gather x6 -> x0, blocking collectives: 47 us -> none  [stacked_from(): pieces = lax.all_gather(pieces, axes[k], axis=0, tiled=True)]
    all_to_all x0 -> x6, blocking collectives: none -> 44.2 us  [stacked_from(): blocks = lax.all_to_all(blocks, axes[k], split_axis=0, concat_axis=0)]
    all_gather x2 -> x0, waiting for transfers between devices: 35.6 us -> none  [stacked_from(): pieces = lax.all_gather(pieces, axes[k], axis=0, tiled=True)]
    all_to_all x0 -> x2, waiting for transfers between devices: none -> 28.3 us  [stacked_from(): blocks = lax.all_to_all(blocks, axes[k], split_axis=0, concat_axis=0)]
    all_to_all x0 -> x2, starting transfers between devices: none -> 8.07 us  [stacked_from(): blocks = lax.all_to_all(blocks, axes[k], split_axis=0, concat_axis=0)]
  transfers between devices with their start and end apart: 4 -> 4, of which waited for: 2 -> 3; matrix products, arithmetic and copies ran while one was open for 3% -> 4% of each run, Pallas kernels for 0% -> 0%
where the time goes in v1:
time: 278 us; the launch traced here: 277 us
  blocking collectives  172 us (62%)
  waiting for transfers between devices  42.6 us (15%)
  matrix products  17.3 us (6%)
  between operations  14.3 us (5%)
  starting transfers between devices  11.8 us (4%)
  local copies, waits for them, and re-layouts  11.7 us (4%)
  other arithmetic  7.55 us (3%)
    all_to_all x1, blocking collectives, sent_and_summed(): lax.all_to_all(pieces, axis, split_axis=0, concat_axis=0, tiled=True)  80.9 us
    all_to_all x2, blocking collectives, sent_to_all(): lax.all_to_all(jnp.broadcast_to(value[None], (devices, *value.shape)), ax...  46.6 us
    all_to_all x6, blocking collectives, stacked_from(): blocks = lax.all_to_all(blocks, axes[k], split_axis=0, concat_axis=0)  44.2 us
    all_to_all x2, waiting for transfers between devices, stacked_from(): blocks = lax.all_to_all(blocks, axes[k], split_axis=0, concat_axis=0)  28.3 us
    all_to_all x1, waiting for transfers between devices, sum_at_owner(): lax.all_to_all(split_up(value, dim, devices), axis, 0, 0, tiled=True)  14.2 us
    dot_general x1, matrix products, per_device(): jnp.dot(errors, weights, preferred_element_type=jnp.float32) * logit_scale  9.42 us
    all_to_all x2, starting transfers between devices, stacked_from(): blocks = lax.all_to_all(blocks, axes[k], split_axis=0, concat_axis=0)  8.07 us
  transfers between devices with their start and end apart: 4, of which 3 were waited for; matrix products, arithmetic and copies ran while one was open for 4% of the time, Pallas kernels for 0%

profile of v1, /device:TPU:32, one launch (start us, length us, event | category | flops | bytes accessed | tf_op | source)
XLA Modules:
  0.0 276.9 jit_solution(8394974163799944045)
XLA Ops:
  7.2 0.7 pad_add_fusion.1
  7.9 5.9 %all_to_all.60 = s32[2,1,8]{2,1,0:T(1,128)S(1)} all-to-all(s32[2,1,8]{2,1,0:T(1,128)S(1)} %pad_add_fusion.1), channel_id=1, replica_groups=mesh['rep'=4,'tok_0'=2,'tok_1'=2,'voc_0'=4,'voc_1'=4] {'tok_0'}, dimensions={0} | all-to-all | bytes 128 | tf_op jit(solution)/shard_map/all_to_all | solution.py:26
  13.8 8.3 %all_to_all.61 = s32[4,2,8]{2,1,0:T(2,128)S(1)} all-to-all(s32[4,2,8]{2,1,0:T(2,128)S(1)} %stack.29), channel_id=1, replica_groups=mesh['rep'=4,'tok_0'=2,'tok_1'=2,'voc_0'=4,'voc_1'=4] {'voc_0'}, dimensions={0} | all-to-all | bytes 512 | tf_op jit(solution)/shard_map/all_to_all | solution.py:26
  22.2 0.6 stack.30
  22.8 4.5 %all-to-all-start.6 = ((s32[4,8,8]{1,2,0:T(8,128)}), s32[4,8,8]{1,2,0:T(8,128)S(1)}, u32[]{:S(2)}, u32[]{:S(2)}) async-start(s32[4,8,8]{1,2,0:T(8,128)} %stack.30), calls=%async_computation.6 | async-start | bytes 32768 | tf_op jit(solution)/shard_map/all_to_all | solution.py:26
  27.3 0.9 pad_maximum_fusion.1
  28.2 4.4 %all-to-all-done.6 = s32[4,8,8]{1,2,0:T(8,128)S(1)} async-done(((s32[4,8,8]{1,2,0:T(8,128)}), s32[4,8,8]{1,2,0:T(8,128)S(1)}, u32[]{:S(2)}, u32[]{:S(2)}) %all-to-all-start.6) | async-done | bytes 1056 | tf_op jit(solution)/shard_map/all_to_all | solution.py:26
  32.8 3.7 %all_to_all.62 = s32[2,1,256]{2,1,0:T(1,128)S(1)} all-to-all(s32[2,1,256]{2,1,0:T(1,128)S(1)} %reshape.80), channel_id=1, replica_groups=mesh['rep'=4,'tok_0'=2,'tok_1'=2,'voc_0'=4,'voc_1'=4] {'tok_1'}, dimensions={0} | all-to-all | bytes 4096 | tf_op jit(solution)/shard_map/all_to_all | solution.py:26
  36.5 7.0 %all_to_all.63 = bf16[2,1,8,4096]{3,2,1,0:T(8,128)(2,1)S(1)} all-to-all(bf16[2,1,8,4096]{3,2,1,0:T(8,128)(2,1)S(1)} %pad_maximum_fusion.1), channel_id=1, replica_groups=mesh['rep'=4,'tok_0'=2,'tok_1'=2,'voc_0'=4,'voc_1'=4] {'tok_0'}, dimensions={0} | all-to-all | bytes 262144 | tf_op jit(solution)/shard_map/all_to_all | solution.py:26
  43.6 11.9 %all_to_all.64 = bf16[4,2,8,4096]{3,2,1,0:T(8,128)(2,1)S(1)} all-to-all(bf16[4,2,8,4096]{3,2,1,0:T(8,128)(2,1)S(1)} %stack.25), channel_id=1, replica_groups=mesh['rep'=4,'tok_0'=2,'tok_1'=2,'voc_0'=4,'voc_1'=4] {'voc_0'}, dimensions={0} | all-to-all | bytes 1048576 | tf_op jit(solution)/shard_map/all_to_all | solution.py:26
  55.5 1.6 stack.26
  57.0 3.6 %all-to-all-start.2 = ((bf16[4,8,8,4096]{3,2,1,0:T(8,128)(2,1)}), bf16[4,8,8,4096]{3,2,1,0:T(8,128)(2,1)S(1)}, u32[]{:S(2)}, u32[]{:S(2)}) async-start(bf16[4,8,8,4096]{3,2,1,0:T(8,128)(2,1)} %stack.26), calls=%async_computation.2 | async-start | bytes 4194304 | tf_op jit(solution)/shard_map/all_to_all | solution.py:26
  61.2 0.7 reduce
  62.2 23.9 %all-to-all-done.2 = bf16[4,8,8,4096]{3,2,1,0:T(8,128)(2,1)S(1)} async-done(((bf16[4,8,8,4096]{3,2,1,0:T(8,128)(2,1)}), bf16[4,8,8,4096]{3,2,1,0:T(8,128)(2,1)S(1)}, u32[]{:S(2)}, u32[]{:S(2)}) %all-to-all-start.2) | async-done | bytes 2097184 | tf_op jit(solution)/shard_map/all_to_all | solution.py:26
  86.4 7.4 %all_to_all.65 = bf16[2,32,8,4096]{3,2,1,0:T(8,128)(2,1)S(1)} all-to-all(bf16[2,32,8,4096]{3,2,1,0:T(8,128)(2,1)S(1)} %pad_maximum_fusion), channel_id=1, replica_groups=mesh['rep'=4,'tok_0'=2,'tok_1'=2,'voc_0'=4,'voc_1'=4] {'tok_1'}, dimensions={0} | all-to-all | bytes 8388608 | tf_op jit(solution)/shard_map/all_to_all | solution.py:26
  94.3 3.2 %slice-done.1 = s8[4194304]{0:T(1024)(128)(4,1)S(1)} async-done(((s8[8388608]{0:T(1024)(128)(4,1)}), s8[4194304]{0:T(1024)(128)(4,1)S(1)}, s32[]{:S(2)}) %slice-start.1) | async-done | bytes 4194328
  97.5 4.6 %multiply_reduce_fusion = (f32[512]{0:T(512)S(1)}, f32[512,1024]{1,0:T(8,128)S(1)}) fusion(bf16[512,4096]{1,0:T(8,128)(2,1)S(1)} %bitcast.61, bf16[1,1024,4096]{2,1,0:T(8,128)(2,1)S(1)} %bitcast.75), kind=kOutput, calls=%fused_computation.16 | convolution fusion | flops 4296015360 | bytes 14682112 | tf_op jit(solution)/shard_map/td,vd->tv/dot_general | solution.py:125
  102.2 0.9 exponential_reduce_fusion
  103.2 16.1 %all_to_all.66 = f32[64,3,512]{2,1,0:T(4,128)S(1)} all-to-all(f32[64,3,512]{2,1,0:T(4,128)S(1)} %broadcast_in_dim.13), channel_id=1, replica_groups=mesh['rep'=4,'tok_0'=2,'tok_1'=2,'voc_0'=4,'voc_1'=4] {'tok_0','tok_1','..., dimensions={0} | all-to-all | bytes 786432 | tf_op jit(solution)/shard_map/all_to_all | solution.py:40
  120.2 0.6 fusion.9
  120.8 9.4 %multiply_convert_fusion = bf16[512,4096]{1,0:T(8,128)(2,1)} fusion(bf16[512,1024]{1,0:T(8,128)(2,1)S(1)} %fusion.9, bf16[1,1024,4096]{2,1,0:T(8,128)(2,1)} %param.7), kind=kOutput, calls=%fused_computation.4 | convolution fusion | flops 4299161600 | bytes 13631488 | tf_op jit(solution)/shard_map/dot_general | solution.py:142
  130.3 3.3 %fusion.6 = f32[128,4096]{1,0:T(8,128)S(1)} fusion(bf16[512,4096]{1,0:T(8,128)(2,1)} %bitcast.62, bf16[1,1024,4096]{2,1,0:T(8,128)(2,1)} %param.7, bf16[512,1024]{1,0:T(8,128)(2,1)S(1)} %fusion.9), kind=kOutput, calls=%fused_computation.6 | convolution fusion | flops 538443776 | bytes 7471104 | tf_op jit(solution)/shard_map/tv,td->vd/dot_general | solution.py:151
  133.8 80.9 %all_to_all.67 = f32[4,128,1024]{2,1,0:T(8,128)S(1)} all-to-all(f32[4,128,1024]{2,1,0:T(8,128)S(1)} %bitcast.65), channel_id=1, replica_groups=mesh['rep'=4,'tok_0'=2,'tok_1'=2,'voc_0'=4,'voc_1'=4] {'rep'}, dimensions={0} | all-to-all | bytes 4194304 | tf_op jit(solution)/shard_map/all_to_all | solution.py:89
  214.9 0.8 copy-done.1
  215.7 2.2 fusion.13
  218.1 30.5 %all_to_all.68 = bf16[4,128,1024]{2,1,0:T(8,128)(2,1)S(1)} all-to-all(bf16[4,128,1024]{2,1,0:T(8,128)(2,1)S(1)} %broadcast_in_dim.28), channel_id=1, replica_groups=mesh['rep'=4,'tok_0'=2,'tok_1'=2,'voc_0'=4,'voc_1'=4] {'rep'}, dimensions={0} | all-to-all | bytes 2097152 | tf_op jit(solution)/shard_map/all_to_all | solution.py:40
  248.5 3.7 %all-to-all-start.9 = ((bf16[16,8,4096]{2,1,0:T(8,128)(2,1)}), bf16[16,8,4096]{2,1,0:T(8,128)(2,1)S(1)}, u32[]{:S(2)}, u32[]{:S(2)}) async-start(bf16[16,8,4096]{2,1,0:T(8,128)(2,1)} %bitcast.70), calls=%async_computation.10 | async-start | bytes 2097152 | tf_op jit(solution)/shard_map/all_to_all | solution.py:83
  252.5 0.6 dynamic-slice_bitcast_fusion
  253.1 0.7 copy.44
  253.8 1.3 copy.45
  255.1 14.2 %all-to-all-done.9 = bf16[16,8,4096]{2,1,0:T(8,128)(2,1)S(1)} async-done(((bf16[16,8,4096]{2,1,0:T(8,128)(2,1)}), bf16[16,8,4096]{2,1,0:T(8,128)(2,1)S(1)}, u32[]{:S(2)}, u32[]{:S(2)}) %all-to-all-start.9) | async-done | bytes 1048608 | tf_op jit(solution)/shard_map/all_to_all | solution.py:83
  269.3 0.8 convert_reduce_fusion
  (76 shorter events, 3.7 us)
Async XLA Ops:
  22.8 9.8 %all-to-all-start.6 = ((s32[4,8,8]{1,2,0:T(8,128)}), s32[4,8,8]{1,2,0:T(8,128)S(1)}, u32[]{:S(2)}, u32[]{:S(2)}) async-start(s32[4,8,8]{1,2,0:T(8,128)} %stack.30), calls=%async_computation.6 | async-start | bytes 32768 | tf_op jit(solution)/shard_map/all_to_all | solution.py:26
  57.0 29.0 %all-to-all-start.2 = ((bf16[4,8,8,4096]{3,2,1,0:T(8,128)(2,1)}), bf16[4,8,8,4096]{3,2,1,0:T(8,128)(2,1)S(1)}, u32[]{:S(2)}, u32[]{:S(2)}) async-start(bf16[4,8,8,4096]{3,2,1,0:T(8,128)(2,1)} %stack.26), calls=%async_computation.2 | async-start | bytes 4194304 | tf_op jit(solution)/shard_map/all_to_all | solution.py:26
  60.6 187.9 %reduce-scatter.2.cloned.1.call-start = ((), (), s32[]{:S(2)}) async-start(), calls=%async_computation.13 | async-start | bytes 5242880 | tf_op jit(solution)/shard_map/reduce_scatter | solution.py:145
  86.4 7.9 %slice-start = ((s8[8388608]{0:T(1024)(128)(4,1)}), s8[4194304]{0:T(1024)(128)(4,1)S(1)}, s32[]{:S(2)}) async-start(s8[8388608]{0:T(1024)(128)(4,1)} %bitcast.74), calls=%async_computation.14 | async-start | bytes 8388608
  93.8 3.7 %slice-start.1 = ((s8[8388608]{0:T(1024)(128)(4,1)}), s8[4194304]{0:T(1024)(128)(4,1)S(1)}, s32[]{:S(2)}) async-start(s8[8388608]{0:T(1024)(128)(4,1)} %bitcast.74), calls=%async_computation.15 | async-start | bytes 8388608
  94.3 7.8 %copy-start = (bf16[2,2,4,4,8,4096]{5,4,3,2,1,0:T(8,128)(2,1)}, bf16[2,2,4,4,8,4096]{5,4,3,2,1,0:T(8,128)(2,1)S(1)}, u32[]{:S(2)}) copy-start(bf16[2,2,4,4,8,4096]{5,4,3,2,1,0:T(8,128)(2,1)S(1)} %copy.37) | copy-start | bytes 12582916
  214.7 1.0 copy-start.1
  248.5 20.8 %all-to-all-start.9 = ((bf16[16,8,4096]{2,1,0:T(8,128)(2,1)}), bf16[16,8,4096]{2,1,0:T(8,128)(2,1)S(1)}, u32[]{:S(2)}, u32[]{:S(2)}) async-start(bf16[16,8,4096]{2,1,0:T(8,128)(2,1)} %bitcast.70), calls=%async_computation.10 | async-start | bytes 2097152 | tf_op jit(solution)/shard_map/all_to_all | solution.py:83
Sparse Core Ops, SparseCore 0:
  130.4 90.9 reduce-scatter.1
